TPU v7x, 32 devices: a whole 2x2x4 slice. The times are simulated.
32 devices in a mesh: colour: 2 (over core), sub: 16 (over z, y, x).
Axes of the slice: x: 2, y: 2, z: 4, core: 2. Of those that a mesh axis runs over, the one named last changes fastest.
Arguments:
- rhs: float32 [3, 64, 256, 512], P(None, 'sub'), may hold values from -60 to 60
- diagonal: float32 [64, 256, 512], P('sub'), may hold values from 0.2 to 6
Outputs:
- solution: float32 [3, 64, 256, 512], P(None, 'sub', None, 'colour')
- residual: float32 [3, 64, 256, 512], P(None, 'sub', None, 'colour')
- norms: float32 [3], replicated
All inputs are finite; a program needn't handle non-finite values.
Results may differ from a plain program's by a relative error of at most 0.0003.
Values sent between devices are 32-bit elements; how exact they have to be, the bound alone decides.
A program may use at most 128 MiB of HBM per device.

v0:
```python
import jax
import jax.numpy as jnp
from jax import lax
from jax.sharding import PartitionSpec as P

CX = 4
NY = 256
NZ = 512
RIM = 1
SWEEPS = 8
BATCH = 1
MICRO = 3


OMEGA = 0.8


def extended_2(block, sides, width):
    for axis, dim in sides:
        count = lax.axis_size(axis)
        forward = [(i, i + 1) for i in range(count - 1)]
        backward = [(target, source) for source, target in forward]
        low = lax.ppermute(
            lax.slice_in_dim(block, block.shape[dim] - width, None, axis=dim), axis, forward
        )
        high = lax.ppermute(lax.slice_in_dim(block, 0, width, axis=dim), axis, backward)
        block = jnp.concatenate([low, block, high], axis=dim)
    return block


def swapped(value, axis, apart):
    mask = 2**apart
    pairs = [(source, source ^ mask) for source in range(lax.axis_size(axis))]
    return lax.ppermute(value, axis, pairs)


def bordered(extended, xpad, zpad):
    padded = jnp.pad(extended, ((0, 0), (xpad, xpad), (1, 1), (zpad, zpad)))
    beside = padded[:, 2:, 1:-1, 1:-1] + padded[:, :-2, 1:-1, 1:-1]
    beside = beside + padded[:, 1:-1, 2:, 1:-1] + padded[:, 1:-1, :-2, 1:-1]
    beside = beside + padded[:, 1:-1, 1:-1, 2:] + padded[:, 1:-1, 1:-1, :-2]
    return beside


def jacobi(resid, diag, mask):
    scale = OMEGA / (6.0 + diag)
    found = jnp.zeros_like(resid)
    for sweep in range(SWEEPS):
        beside = bordered(found, 1, 1)
        found = (found + scale * (resid - (6.0 + diag) * found + beside)) * mask
    return found


def slab_operator(field, diagonal):
    extended = extended_2(field, (("sub", 1),), 1)
    sides = bordered(extended, 0, 1)
    return (6.0 + diagonal) * field - sides


def colour_step(current, resid, diagonal, diag_rim, colour, device, total):
    half = CX // 2
    span = half + 2 * RIM
    offset = colour * half
    padded_resid = extended_2(resid, (("sub", 1),), RIM)
    region_resid = lax.dynamic_slice_in_dim(padded_resid, offset, span, 1)
    region_diag = lax.dynamic_slice_in_dim(diag_rim, offset, span, 0)
    place = device * CX + offset - RIM + lax.iota(jnp.int32, span)
    mask = ((place >= 0) & (place < total)).astype(jnp.float32)[:, None, None]
    found = jacobi(region_resid * mask, region_diag, mask)
    placed = jnp.zeros((resid.shape[0], CX + 2 * RIM, resid.shape[2], resid.shape[3]), jnp.float32)
    placed = lax.dynamic_update_slice_in_dim(placed, found, offset, 1)
    outgoing = jnp.concatenate([placed[:, :RIM], placed[:, CX + RIM :]], axis=1)
    arrived = extended_2(outgoing, (("sub", 1),), RIM)
    from_left = jnp.pad(arrived[:, :RIM], ((0, 0), (0, CX - RIM), (0, 0), (0, 0)))
    from_right = jnp.pad(arrived[:, 3 * RIM :], ((0, 0), (CX - RIM, 0), (0, 0), (0, 0)))
    correction = placed[:, RIM : RIM + CX] + from_left + from_right
    image = slab_operator(correction, diagonal)
    upper_part = jnp.sum(resid * correction, axis=(1, 2, 3))
    lower_part = jnp.sum(correction * image, axis=(1, 2, 3))
    upper, lower = lax.psum((upper_part, lower_part), "sub")
    alpha = (upper / lower)[:, None, None, None]
    return (current + alpha * correction, resid - alpha * image)


def shards(rhs, diagonal):
    colour = lax.axis_index("colour")
    device = lax.axis_index("sub")
    total = lax.axis_size("sub") * CX
    diag_rim = extended_2(diagonal, (("sub", 0),), RIM)
    half_z = NZ // 2
    lower_z = colour * half_z
    sol_parts = []
    res_parts = []
    blank = jnp.zeros((BATCH, CX, NY, NZ), jnp.float32)
    carry_u = blank
    carry_r = rhs[:BATCH]
    first = colour == 0
    for step in range(MICRO + 1):
        section_batch = jnp.clip(step - colour, 0, MICRO - 1)
        source = lax.dynamic_slice_in_dim(rhs, section_batch * BATCH, BATCH, 0)
        current = jnp.where(first, blank, carry_u)
        resid = jnp.where(first, source, carry_r)
        new_u, new_r = colour_step(current, resid, diagonal, diag_rim, colour, device, total)
        got_u, got_r = swapped((new_u, new_r), "colour", 0)
        carry_u = got_u
        carry_r = got_r
        if step >= 1:
            done_u = jnp.where(first, got_u, new_u)
            done_r = jnp.where(first, got_r, new_r)
            part_u = lax.dynamic_slice_in_dim(done_u, lower_z, half_z, 3)
            part_r = lax.dynamic_slice_in_dim(done_r, lower_z, half_z, 3)
            sol_parts.append(part_u)
            res_parts.append(part_r)
    solution = jnp.concatenate(sol_parts, axis=0)
    residual = jnp.concatenate(res_parts, axis=0)
    squares = lax.psum(jnp.sum(residual * residual, axis=(1, 2, 3)), ("colour", "sub"))
    return (solution, residual, jnp.sqrt(squares))


def solution(mesh):
    placed = (P(None, "sub", None, None), P("sub", None, None))
    return jax.shard_map(
        shards,
        mesh=mesh,
        in_specs=placed,
        out_specs=(P(None, "sub", None, "colour"), P(None, "sub", None, "colour"), P()),
        check_vma=False,
    )
```

profile of v0, /device:TPU:10, one launch (start us, length us, event | category | flops | bytes accessed | tf_op | source)
XLA Modules:
  0.0 708.1 jit_solution(10036438138919230028)
XLA Ops:
  1.9 3.4 collective-permute-start
  7.8 2.7 slice_select_fusion
  11.9 4.3 collective-permute-start.2
  18.2 22.9 %collective-permute-done = f32[1,256,512]{2,1,0:T(8,128)S(1)} collective-permute-done((f32[1,256,512]{2,1,0:T(8,128)S(1)}, f32[1,256,512]{2,1,0:T(8,128)S(1)}, u32[]{:S(2)}, u32[]{:S(2)}) %collective-permute-start) | collective-permute-done | bytes 524320 | tf_op jit(solution)/shard_map/ppermute | solution.py:23
  41.1 10.2 %collective-permute-done.2 = f32[1,1,256,512]{3,2,1,0:T(8,128)} collective-permute-done((f32[1,1,256,512]{3,2,1,0:T(8,128)S(1)}, f32[1,1,256,512]{3,2,1,0:T(8,128)}, u32[]{:S(2)}, u32[]{:S(2)}) %collective-permute-start.2) | collective-permute-done | bytes 524320 | tf_op jit(solution)/shard_map/ppermute | solution.py:23
  52.5 4.5 fusion.321
  74.3 3.3 collective-permute-start.4
  77.6 2.8 collective-permute-start.5
  80.4 19.7 %collective-permute-done.4 = f32[1,1,256,512]{3,2,1,0:T(8,128)S(1)} collective-permute-done((f32[1,1,256,512]{3,2,1,0:T(8,128)S(1)}, f32[1,1,256,512]{3,2,1,0:T(8,128)S(1)}, u32[]{:S(2)}, u32[]{:S(2)}) %collective-permute-start.4) | collective-permute-done | bytes 524320 | tf_op jit(solution)/shard_map/ppermute | solution.py:23
  101.3 3.6 collective-permute-start.7
  104.8 2.9 collective-permute-start.6
  107.7 19.8 %collective-permute-done.7 = f32[1,1,256,512]{3,2,1,0:T(8,128)S(1)} collective-permute-done((f32[1,1,256,512]{3,2,1,0:T(8,128)S(1)}, f32[1,1,256,512]{3,2,1,0:T(8,128)S(1)}, u32[]{:S(2)}, u32[]{:S(2)}) %collective-permute-start.7) | collective-permute-done | bytes 524320 | tf_op jit(solution)/shard_map/ppermute | solution.py:23
  130.5 4.0 multiply_reduce_fusion.7
  134.5 32.9 %all-reduce.44 = (f32[1]{0:T(128)}, f32[1]{0:T(128)}) all-reduce(f32[1]{0:T(128)} %bitcast.3, f32[1]{0:T(128)} %bitcast.5), channel_id=1, replica_groups=mesh['colour'=2,'sub'=16] {'sub'}, use_global_device_ids=true, to_apply=%region_1.2 | all-reduce | flops 2 | bytes 16 | tf_op jit(solution)/shard_map/psum | solution.py:80
  168.7 5.0 multiply_subtract_fusion.3
  173.7 4.5 collective-permute-done.9
  183.0 4.6 collective-permute-start.11
  187.6 22.0 %collective-permute-done.10 = f32[1,1,256,512]{3,2,1,0:T(8,128)S(1)} collective-permute-done((f32[1,1,256,512]{3,2,1,0:T(8,128)S(1)}, f32[1,1,256,512]{3,2,1,0:T(8,128)S(1)}, u32[]{:S(2)}, u32[]{:S(2)}) %collective-permute-start.10) | collective-permute-done | bytes 524320 | tf_op jit(solution)/shard_map/ppermute | solution.py:23
  229.3 3.7 collective-permute-start.12
  235.1 21.2 %collective-permute-done.12 = f32[1,1,256,512]{3,2,1,0:T(8,128)S(1)} collective-permute-done((f32[1,1,256,512]{3,2,1,0:T(8,128)S(1)}, f32[1,1,256,512]{3,2,1,0:T(8,128)S(1)}, u32[]{:S(2)}, u32[]{:S(2)}) %collective-permute-start.12) | collective-permute-done | bytes 524320 | tf_op jit(solution)/shard_map/ppermute | solution.py:23
  257.4 3.3 collective-permute-start.15
  260.7 2.8 collective-permute-start.14
  263.6 20.0 %collective-permute-done.15 = f32[1,1,256,512]{3,2,1,0:T(8,128)S(1)} collective-permute-done((f32[1,1,256,512]{3,2,1,0:T(8,128)S(1)}, f32[1,1,256,512]{3,2,1,0:T(8,128)S(1)}, u32[]{:S(2)}, u32[]{:S(2)}) %collective-permute-start.15) | collective-permute-done | bytes 524320 | tf_op jit(solution)/shard_map/ppermute | solution.py:23
  286.3 3.8 multiply_reduce_fusion.5
  290.1 35.5 %all-reduce.43 = (f32[1]{0:T(128)}, f32[1]{0:T(128)}) all-reduce(f32[1]{0:T(128)} %bitcast.7, f32[1]{0:T(128)} %bitcast.8), channel_id=1, replica_groups=mesh['colour'=2,'sub'=16] {'sub'}, use_global_device_ids=true, to_apply=%region_5.6 | all-reduce | flops 2 | bytes 16 | tf_op jit(solution)/shard_map/psum | solution.py:80
  326.9 4.1 multiply_subtract_fusion.2
  331.0 4.5 collective-permute-done.17
  339.8 4.1 collective-permute-start.19
  344.0 22.0 %collective-permute-done.18 = f32[1,1,256,512]{3,2,1,0:T(8,128)S(1)} collective-permute-done((f32[1,1,256,512]{3,2,1,0:T(8,128)S(1)}, f32[1,1,256,512]{3,2,1,0:T(8,128)S(1)}, u32[]{:S(2)}, u32[]{:S(2)}) %collective-permute-start.18) | collective-permute-done | bytes 524320 | tf_op jit(solution)/shard_map/ppermute | solution.py:23
  385.6 3.0 collective-permute-start.20
  388.7 2.8 collective-permute-start.21
  391.5 21.2 %collective-permute-done.20 = f32[1,1,256,512]{3,2,1,0:T(8,128)S(1)} collective-permute-done((f32[1,1,256,512]{3,2,1,0:T(8,128)S(1)}, f32[1,1,256,512]{3,2,1,0:T(8,128)S(1)}, u32[]{:S(2)}, u32[]{:S(2)}) %collective-permute-start.20) | collective-permute-done | bytes 524320 | tf_op jit(solution)/shard_map/ppermute | solution.py:23
  413.7 3.4 collective-permute-start.23
  417.2 3.0 collective-permute-start.22
  420.1 19.8 %collective-permute-done.23 = f32[1,1,256,512]{3,2,1,0:T(8,128)S(1)} collective-permute-done((f32[1,1,256,512]{3,2,1,0:T(8,128)S(1)}, f32[1,1,256,512]{3,2,1,0:T(8,128)S(1)}, u32[]{:S(2)}, u32[]{:S(2)}) %collective-permute-start.23) | collective-permute-done | bytes 524320 | tf_op jit(solution)/shard_map/ppermute | solution.py:23
  442.8 3.8 multiply_reduce_fusion.3
  446.6 35.5 %all-reduce.42 = (f32[1]{0:T(128)}, f32[1]{0:T(128)}) all-reduce(f32[1]{0:T(128)} %bitcast.10, f32[1]{0:T(128)} %bitcast.11), channel_id=1, replica_groups=mesh['colour'=2,'sub'=16] {'sub'}, use_global_device_ids=true, to_apply=%region_9.10 | all-reduce | flops 2 | bytes 16 | tf_op jit(solution)/shard_map/psum | solution.py:80
  483.4 4.2 multiply_subtract_fusion.1
  496.6 4.2 collective-permute-start.27
  503.7 19.0 %collective-permute-done.26 = f32[1,1,256,512]{3,2,1,0:T(8,128)S(1)} collective-permute-done((f32[1,1,256,512]{3,2,1,0:T(8,128)S(1)}, f32[1,1,256,512]{3,2,1,0:T(8,128)S(1)}, u32[]{:S(2)}, u32[]{:S(2)}) %collective-permute-start.26) | collective-permute-done | bytes 524320 | tf_op jit(solution)/shard_map/ppermute | solution.py:23
  542.4 3.2 collective-permute-start.28
  548.2 21.2 %collective-permute-done.28 = f32[1,1,256,512]{3,2,1,0:T(8,128)S(1)} collective-permute-done((f32[1,1,256,512]{3,2,1,0:T(8,128)S(1)}, f32[1,1,256,512]{3,2,1,0:T(8,128)S(1)}, u32[]{:S(2)}, u32[]{:S(2)}) %collective-permute-start.28) | collective-permute-done | bytes 524320 | tf_op jit(solution)/shard_map/ppermute | solution.py:23
  570.0 3.7 collective-permute-start.31
  578.2 18.1 %collective-permute-done.31 = f32[1,1,256,512]{3,2,1,0:T(8,128)S(1)} collective-permute-done((f32[1,1,256,512]{3,2,1,0:T(8,128)S(1)}, f32[1,1,256,512]{3,2,1,0:T(8,128)S(1)}, u32[]{:S(2)}, u32[]{:S(2)}) %collective-permute-start.31) | collective-permute-done | bytes 524320 | tf_op jit(solution)/shard_map/ppermute | solution.py:23
  599.3 2.8 multiply_reduce_fusion.1
  602.0 35.5 %all-reduce.41 = (f32[1]{0:T(128)}, f32[1]{0:T(128)}) all-reduce(f32[1]{0:T(128)} %bitcast.13, f32[1]{0:T(128)} %bitcast.14), channel_id=1, replica_groups=mesh['colour'=2,'sub'=16] {'sub'}, use_global_device_ids=true, to_apply=%region_13.14 | all-reduce | flops 2 | bytes 16 | tf_op jit(solution)/shard_map/psum | solution.py:80
  638.8 3.6 multiply_subtract_fusion
  656.7 47.0 %psum.71 = f32[3]{0:T(128)S(1)} all-reduce(f32[3]{0:T(128)S(1)} %get-tuple-element.19), channel_id=1, replica_groups=mesh['colour'=2,'sub'=16] {'colour','sub'}, use_global_device_ids=true, to_apply=%region_17.18 | all-reduce | flops 3 | bytes 24 | tf_op jit(solution)/shard_map/psum | solution.py:116
  (178 shorter events, 147.9 us)
Async XLA Ops:
  1.9 39.2 %collective-permute-start = (f32[1,256,512]{2,1,0:T(8,128)S(1)}, f32[1,256,512]{2,1,0:T(8,128)S(1)}, u32[]{:S(2)}, u32[]{:S(2)}) collective-permute-start(f32[1,256,512]{2,1,0:T(8,128)S(1)} %get-tuple-element.58), channel_id=1, source_target_pairs={{0,1},{1,2},{2,3},{3,4},{4,5},{5,6},{6,7},{7,8},{8,9},{9,10},{10,1... | collective-permute-start | bytes 1572872 | tf_op jit(solution)/shard_map/ppermute | solution.py:23
  5.3 35.8 %collective-permute-start.1 = (f32[1,256,512]{2,1,0:T(8,128)S(1)}, f32[1,256,512]{2,1,0:T(8,128)S(1)}, u32[]{:S(2)}, u32[]{:S(2)}) collective-permute-start(f32[1,256,512]{2,1,0:T(8,128)S(1)} %get-tuple-element.59), channel_id=1, source_target_pairs={{1,0},{2,1},{3,2},{4,3},{5,4},{6,5},{7,6},{8,7},{9,8},{10,9},{11,1... | collective-permute-start | bytes 1572872 | tf_op jit(solution)/shard_map/ppermute | solution.py:26
  11.9 39.4 %collective-permute-start.2 = (f32[1,1,256,512]{3,2,1,0:T(8,128)S(1)}, f32[1,1,256,512]{3,2,1,0:T(8,128)}, u32[]{:S(2)}, u32[]{:S(2)}) collective-permute-start(f32[1,1,256,512]{3,2,1,0:T(8,128)S(1)} %get-tuple-element.56), channel_id=1, source_target_pairs={{0,1},{1,2},{2,3},{3,4},{4,5},{5,6},{6,7},{7,8},{8,9},{9,10},{10,1... | collective-permute-start | bytes 1572872 | tf_op jit(solution)/shard_map/ppermute | solution.py:23
  16.2 36.0 %collective-permute-start.3 = (f32[1,1,256,512]{3,2,1,0:T(8,128)S(1)}, f32[1,1,256,512]{3,2,1,0:T(8,128)}, u32[]{:S(2)}, u32[]{:S(2)}) collective-permute-start(f32[1,1,256,512]{3,2,1,0:T(8,128)S(1)} %get-tuple-element.57), channel_id=1, source_target_pairs={{1,0},{2,1},{3,2},{4,3},{5,4},{6,5},{7,6},{8,7},{9,8},{10,9},{11,1... | collective-permute-start | bytes 1572872 | tf_op jit(solution)/shard_map/ppermute | solution.py:26
  18.1 34.4 %copy-start.20 = (f32[1,4,256,512]{3,2,1,0:T(8,128)S(1)}, f32[1,4,256,512]{3,2,1,0:T(8,128)}, u32[]{:S(2)}) copy-start(f32[1,4,256,512]{3,2,1,0:T(8,128)} %copy-done.19) | copy-start | bytes 6291460
  71.8 58.7 %slice-start = ((s8[6291456]{0:T(1024)(128)(4,1)}), s8[2097152]{0:T(1024)(128)(4,1)S(1)}, s32[]{:S(2)}) async-start(s8[6291456]{0:T(1024)(128)(4,1)} %bitcast.232), calls=%async_computation | async-start | bytes 4194304
  74.2 27.0 %copy-start.11 = (f32[1,6,256,512]{3,2,1,0:T(8,128)}, f32[1,6,256,512]{3,2,1,0:T(8,128)S(1)}, u32[]{:S(2)}) copy-start(f32[1,6,256,512]{3,2,1,0:T(8,128)S(1)} %fusion.81) | copy-start | bytes 9437188
  74.3 25.9 %collective-permute-start.4 = (f32[1,1,256,512]{3,2,1,0:T(8,128)S(1)}, f32[1,1,256,512]{3,2,1,0:T(8,128)S(1)}, u32[]{:S(2)}, u32[]{:S(2)}) collective-permute-start(f32[1,1,256,512]{3,2,1,0:T(8,128)S(1)} %get-tuple-element.40), channel_id=1, source_target_pairs={{0,1},{1,2},{2,3},{3,4},{4,5},{5,6},{6,7},{7,8},{8,9},{9,10},{10,1... | collective-permute-start | bytes 1572872 | tf_op jit(solution)/shard_map/ppermute | solution.py:23
  77.6 52.9 %slice-start.1 = ((s8[6291456]{0:T(1024)(128)(4,1)}), s8[4194304]{0:T(1024)(128)(4,1)S(1)}, s32[]{:S(2)}) async-start(s8[6291456]{0:T(1024)(128)(4,1)} %bitcast.232), calls=%async_computation.1 | async-start | bytes 8388608
  77.6 23.2 %collective-permute-start.5 = (f32[1,1,256,512]{3,2,1,0:T(8,128)S(1)}, f32[1,1,256,512]{3,2,1,0:T(8,128)S(1)}, u32[]{:S(2)}, u32[]{:S(2)}) collective-permute-start(f32[1,1,256,512]{3,2,1,0:T(8,128)S(1)} %get-tuple-element.41), channel_id=1, source_target_pairs={{1,0},{2,1},{3,2},{4,3},{5,4},{6,5},{7,6},{8,7},{9,8},{10,9},{11,1... | collective-permute-start | bytes 1572872 | tf_op jit(solution)/shard_map/ppermute | solution.py:26
  101.3 26.3 %collective-permute-start.7 = (f32[1,1,256,512]{3,2,1,0:T(8,128)S(1)}, f32[1,1,256,512]{3,2,1,0:T(8,128)S(1)}, u32[]{:S(2)}, u32[]{:S(2)}) collective-permute-start(f32[1,1,256,512]{3,2,1,0:T(8,128)S(1)} %get-tuple-element.54), channel_id=1, source_target_pairs={{0,1},{1,2},{2,3},{3,4},{4,5},{5,6},{6,7},{7,8},{8,9},{9,10},{10,1... | collective-permute-start | bytes 1572872 | tf_op jit(solution)/shard_map/ppermute | solution.py:23
  104.8 25.6 %copy-start = (f32[4,256,512]{2,1,0:T(8,128)S(1)}, f32[4,256,512]{2,1,0:T(8,128)}, u32[]{:S(2)}) copy-start(f32[4,256,512]{2,1,0:T(8,128)} %param.3) | copy-start | bytes 6291460
  104.8 23.3 %collective-permute-start.6 = (f32[1,1,256,512]{3,2,1,0:T(8,128)S(1)}, f32[1,1,256,512]{3,2,1,0:T(8,128)S(1)}, u32[]{:S(2)}, u32[]{:S(2)}) collective-permute-start(f32[1,1,256,512]{3,2,1,0:T(8,128)S(1)} %get-tuple-element.55), channel_id=1, source_target_pairs={{1,0},{2,1},{3,2},{4,3},{5,4},{6,5},{7,6},{8,7},{9,8},{10,9},{11,1... | collective-permute-start | bytes 1572872 | tf_op jit(solution)/shard_map/ppermute | solution.py:26
  173.7 4.5 collective-permute-start.9
  180.3 106.1 %copy-start.9 = (f32[1,4,256,512]{3,2,1,0:T(8,128)}, f32[1,4,256,512]{3,2,1,0:T(8,128)S(1)}, u32[]{:S(2)}) copy-start(f32[1,4,256,512]{3,2,1,0:T(8,128)S(1)} %dynamic-slice_select_fusion.2) | copy-start | bytes 6291460
  180.3 29.3 %copy-start.5 = (f32[1,4,256,512]{3,2,1,0:T(8,128)S(1)}, f32[1,4,256,512]{3,2,1,0:T(8,128)}, u32[]{:S(2)}) copy-start(f32[1,4,256,512]{3,2,1,0:T(8,128)} %copy-done.4) | copy-start | bytes 6291460
  180.4 29.2 %collective-permute-start.10 = (f32[1,1,256,512]{3,2,1,0:T(8,128)S(1)}, f32[1,1,256,512]{3,2,1,0:T(8,128)S(1)}, u32[]{:S(2)}, u32[]{:S(2)}) collective-permute-start(f32[1,1,256,512]{3,2,1,0:T(8,128)S(1)} %get-tuple-element.52), channel_id=1, source_target_pairs={{0,1},{1,2},{2,3},{3,4},{4,5},{5,6},{6,7},{7,8},{8,9},{9,10},{10,1... | collective-permute-start | bytes 1572872 | tf_op jit(solution)/shard_map/ppermute | solution.py:23
  183.0 26.6 %collective-permute-start.11 = (f32[1,1,256,512]{3,2,1,0:T(8,128)S(1)}, f32[1,1,256,512]{3,2,1,0:T(8,128)S(1)}, u32[]{:S(2)}, u32[]{:S(2)}) collective-permute-start(f32[1,1,256,512]{3,2,1,0:T(8,128)S(1)} %get-tuple-element.53), channel_id=1, source_target_pairs={{1,0},{2,1},{3,2},{4,3},{5,4},{6,5},{7,6},{8,7},{9,8},{10,9},{11,1... | collective-permute-start | bytes 1572872 | tf_op jit(solution)/shard_map/ppermute | solution.py:26
  229.2 27.6 %copy-start.15 = (f32[1,6,256,512]{3,2,1,0:T(8,128)}, f32[1,6,256,512]{3,2,1,0:T(8,128)S(1)}, u32[]{:S(2)}) copy-start(f32[1,6,256,512]{3,2,1,0:T(8,128)S(1)} %fusion.145) | copy-start | bytes 9437188
  229.3 27.1 %collective-permute-start.12 = (f32[1,1,256,512]{3,2,1,0:T(8,128)S(1)}, f32[1,1,256,512]{3,2,1,0:T(8,128)S(1)}, u32[]{:S(2)}, u32[]{:S(2)}) collective-permute-start(f32[1,1,256,512]{3,2,1,0:T(8,128)S(1)} %get-tuple-element.38), channel_id=1, source_target_pairs={{0,1},{1,2},{2,3},{3,4},{4,5},{5,6},{6,7},{7,8},{8,9},{9,10},{10,1... | collective-permute-start | bytes 1572872 | tf_op jit(solution)/shard_map/ppermute | solution.py:23
  233.0 23.3 %collective-permute-start.13 = (f32[1,1,256,512]{3,2,1,0:T(8,128)S(1)}, f32[1,1,256,512]{3,2,1,0:T(8,128)S(1)}, u32[]{:S(2)}, u32[]{:S(2)}) collective-permute-start(f32[1,1,256,512]{3,2,1,0:T(8,128)S(1)} %get-tuple-element.39), channel_id=1, source_target_pairs={{1,0},{2,1},{3,2},{4,3},{5,4},{6,5},{7,6},{8,7},{9,8},{10,9},{11,1... | collective-permute-start | bytes 1572872 | tf_op jit(solution)/shard_map/ppermute | solution.py:26
  257.4 26.2 %collective-permute-start.15 = (f32[1,1,256,512]{3,2,1,0:T(8,128)S(1)}, f32[1,1,256,512]{3,2,1,0:T(8,128)S(1)}, u32[]{:S(2)}, u32[]{:S(2)}) collective-permute-start(f32[1,1,256,512]{3,2,1,0:T(8,128)S(1)} %get-tuple-element.50), channel_id=1, source_target_pairs={{0,1},{1,2},{2,3},{3,4},{4,5},{5,6},{6,7},{7,8},{8,9},{9,10},{10,1... | collective-permute-start | bytes 1572872 | tf_op jit(solution)/shard_map/ppermute | solution.py:23
  260.7 23.3 %collective-permute-start.14 = (f32[1,1,256,512]{3,2,1,0:T(8,128)S(1)}, f32[1,1,256,512]{3,2,1,0:T(8,128)S(1)}, u32[]{:S(2)}, u32[]{:S(2)}) collective-permute-start(f32[1,1,256,512]{3,2,1,0:T(8,128)S(1)} %get-tuple-element.51), channel_id=1, source_target_pairs={{1,0},{2,1},{3,2},{4,3},{5,4},{6,5},{7,6},{8,7},{9,8},{10,9},{11,1... | collective-permute-start | bytes 1572872 | tf_op jit(solution)/shard_map/ppermute | solution.py:26
  331.0 4.5 collective-permute-start.17
  337.5 105.2 %copy-start.10 = (f32[1,4,256,512]{3,2,1,0:T(8,128)}, f32[1,4,256,512]{3,2,1,0:T(8,128)S(1)}, u32[]{:S(2)}) copy-start(f32[1,4,256,512]{3,2,1,0:T(8,128)S(1)} %dynamic-slice_select_fusion.1) | copy-start | bytes 6291460
  337.6 28.4 %copy-start.6 = (f32[1,4,256,512]{3,2,1,0:T(8,128)S(1)}, f32[1,4,256,512]{3,2,1,0:T(8,128)}, u32[]{:S(2)}) copy-start(f32[1,4,256,512]{3,2,1,0:T(8,128)} %copy-done.4) | copy-start | bytes 6291460
  337.6 28.3 %collective-permute-start.18 = (f32[1,1,256,512]{3,2,1,0:T(8,128)S(1)}, f32[1,1,256,512]{3,2,1,0:T(8,128)S(1)}, u32[]{:S(2)}, u32[]{:S(2)}) collective-permute-start(f32[1,1,256,512]{3,2,1,0:T(8,128)S(1)} %get-tuple-element.48), channel_id=1, source_target_pairs={{0,1},{1,2},{2,3},{3,4},{4,5},{5,6},{6,7},{7,8},{8,9},{9,10},{10,1... | collective-permute-start | bytes 1572872 | tf_op jit(solution)/shard_map/ppermute | solution.py:23
  339.8 26.1 %collective-permute-start.19 = (f32[1,1,256,512]{3,2,1,0:T(8,128)S(1)}, f32[1,1,256,512]{3,2,1,0:T(8,128)S(1)}, u32[]{:S(2)}, u32[]{:S(2)}) collective-permute-start(f32[1,1,256,512]{3,2,1,0:T(8,128)S(1)} %get-tuple-element.49), channel_id=1, source_target_pairs={{1,0},{2,1},{3,2},{4,3},{5,4},{6,5},{7,6},{8,7},{9,8},{10,9},{11,1... | collective-permute-start | bytes 1572872 | tf_op jit(solution)/shard_map/ppermute | solution.py:26
  385.5 27.6 %copy-start.17 = (f32[1,6,256,512]{3,2,1,0:T(8,128)}, f32[1,6,256,512]{3,2,1,0:T(8,128)S(1)}, u32[]{:S(2)}) copy-start(f32[1,6,256,512]{3,2,1,0:T(8,128)S(1)} %fusion.209) | copy-start | bytes 9437188
  385.6 27.1 %collective-permute-start.20 = (f32[1,1,256,512]{3,2,1,0:T(8,128)S(1)}, f32[1,1,256,512]{3,2,1,0:T(8,128)S(1)}, u32[]{:S(2)}, u32[]{:S(2)}) collective-permute-start(f32[1,1,256,512]{3,2,1,0:T(8,128)S(1)} %get-tuple-element.36), channel_id=1, source_target_pairs={{0,1},{1,2},{2,3},{3,4},{4,5},{5,6},{6,7},{7,8},{8,9},{9,10},{10,1... | collective-permute-start | bytes 1572872 | tf_op jit(solution)/shard_map/ppermute | solution.py:23
  388.7 24.0 %collective-permute-start.21 = (f32[1,1,256,512]{3,2,1,0:T(8,128)S(1)}, f32[1,1,256,512]{3,2,1,0:T(8,128)S(1)}, u32[]{:S(2)}, u32[]{:S(2)}) collective-permute-start(f32[1,1,256,512]{3,2,1,0:T(8,128)S(1)} %get-tuple-element.37), channel_id=1, source_target_pairs={{1,0},{2,1},{3,2},{4,3},{5,4},{6,5},{7,6},{8,7},{9,8},{10,9},{11,1... | collective-permute-start | bytes 1572872 | tf_op jit(solution)/shard_map/ppermute | solution.py:26
  413.7 26.2 %collective-permute-start.23 = (f32[1,1,256,512]{3,2,1,0:T(8,128)S(1)}, f32[1,1,256,512]{3,2,1,0:T(8,128)S(1)}, u32[]{:S(2)}, u32[]{:S(2)}) collective-permute-start(f32[1,1,256,512]{3,2,1,0:T(8,128)S(1)} %get-tuple-element.46), channel_id=1, source_target_pairs={{0,1},{1,2},{2,3},{3,4},{4,5},{5,6},{6,7},{7,8},{8,9},{9,10},{10,1... | collective-permute-start | bytes 1572872 | tf_op jit(solution)/shard_map/ppermute | solution.py:23
  417.2 23.3 %collective-permute-start.22 = (f32[1,1,256,512]{3,2,1,0:T(8,128)S(1)}, f32[1,1,256,512]{3,2,1,0:T(8,128)S(1)}, u32[]{:S(2)}, u32[]{:S(2)}) collective-permute-start(f32[1,1,256,512]{3,2,1,0:T(8,128)S(1)} %get-tuple-element.47), channel_id=1, source_target_pairs={{1,0},{2,1},{3,2},{4,3},{5,4},{6,5},{7,6},{8,7},{9,8},{10,9},{11,1... | collective-permute-start | bytes 1572872 | tf_op jit(solution)/shard_map/ppermute | solution.py:26
  487.6 4.5 collective-permute-start.25
  489.3 11.6 %collective-permute-start.8 = (f32[1,4,256,512]{3,2,1,0:T(8,128)}, f32[1,4,256,512]{3,2,1,0:T(8,128)}, u32[]{:S(2)}, u32[]{:S(2)}) collective-permute-start(f32[1,4,256,512]{3,2,1,0:T(8,128)} %broadcast_multiply_fusion), channel_id=1, source_target_pairs={{0,16},{16,0},{1,17},{17,1},{2,18},{18,2},{3,19},{19,3},{4,20},{20... | collective-permute-start | bytes 6291464 | tf_op jit(solution)/shard_map/ppermute | solution.py:34
  494.3 104.9 %copy-start.8 = (f32[1,4,256,512]{3,2,1,0:T(8,128)}, f32[1,4,256,512]{3,2,1,0:T(8,128)S(1)}, u32[]{:S(2)}) copy-start(f32[1,4,256,512]{3,2,1,0:T(8,128)S(1)} %dynamic-slice_select_fusion) | copy-start | bytes 6291460
  494.4 28.3 %collective-permute-start.26 = (f32[1,1,256,512]{3,2,1,0:T(8,128)S(1)}, f32[1,1,256,512]{3,2,1,0:T(8,128)S(1)}, u32[]{:S(2)}, u32[]{:S(2)}) collective-permute-start(f32[1,1,256,512]{3,2,1,0:T(8,128)S(1)} %get-tuple-element.44), channel_id=1, source_target_pairs={{0,1},{1,2},{2,3},{3,4},{4,5},{5,6},{6,7},{7,8},{8,9},{9,10},{10,1... | collective-permute-start | bytes 1572872 | tf_op jit(solution)/shard_map/ppermute | solution.py:23
  496.6 26.1 %copy-start.7 = (f32[1,4,256,512]{3,2,1,0:T(8,128)S(1)}, f32[1,4,256,512]{3,2,1,0:T(8,128)}, u32[]{:S(2)}) copy-start(f32[1,4,256,512]{3,2,1,0:T(8,128)} %copy-done.4) | copy-start | bytes 6291460
  496.6 26.1 %collective-permute-start.27 = (f32[1,1,256,512]{3,2,1,0:T(8,128)S(1)}, f32[1,1,256,512]{3,2,1,0:T(8,128)S(1)}, u32[]{:S(2)}, u32[]{:S(2)}) collective-permute-start(f32[1,1,256,512]{3,2,1,0:T(8,128)S(1)} %get-tuple-element.45), channel_id=1, source_target_pairs={{1,0},{2,1},{3,2},{4,3},{5,4},{6,5},{7,6},{8,7},{9,8},{10,9},{11,1... | collective-permute-start | bytes 1572872 | tf_op jit(solution)/shard_map/ppermute | solution.py:26
  501.6 74.5 %collective-permute-start.16 = (f32[1,4,256,512]{3,2,1,0:T(8,128)S(1)}, f32[1,4,256,512]{3,2,1,0:T(8,128)S(1)}, u32[]{:S(2)}, u32[]{:S(2)}) collective-permute-start(f32[1,4,256,512]{3,2,1,0:T(8,128)S(1)} %multiply_add_fusion.2), channel_id=1, source_target_pairs={{0,16},{16,0},{1,17},{17,1},{2,18},{18,2},{3,19},{19,3},{4,20},{20... | collective-permute-start | bytes 6291464 | tf_op jit(solution)/shard_map/ppermute | solution.py:34
  542.3 27.6 %copy-start.13 = (f32[1,6,256,512]{3,2,1,0:T(8,128)}, f32[1,6,256,512]{3,2,1,0:T(8,128)S(1)}, u32[]{:S(2)}) copy-start(f32[1,6,256,512]{3,2,1,0:T(8,128)S(1)} %fusion.273) | copy-start | bytes 9437188
  542.4 27.1 %collective-permute-start.28 = (f32[1,1,256,512]{3,2,1,0:T(8,128)S(1)}, f32[1,1,256,512]{3,2,1,0:T(8,128)S(1)}, u32[]{:S(2)}, u32[]{:S(2)}) collective-permute-start(f32[1,1,256,512]{3,2,1,0:T(8,128)S(1)} %get-tuple-element.34), channel_id=1, source_target_pairs={{0,1},{1,2},{2,3},{3,4},{4,5},{5,6},{6,7},{7,8},{8,9},{9,10},{10,1... | collective-permute-start | bytes 1572872 | tf_op jit(solution)/shard_map/ppermute | solution.py:23
  545.6 23.9 %collective-permute-start.29 = (f32[1,1,256,512]{3,2,1,0:T(8,128)S(1)}, f32[1,1,256,512]{3,2,1,0:T(8,128)S(1)}, u32[]{:S(2)}, u32[]{:S(2)}) collective-permute-start(f32[1,1,256,512]{3,2,1,0:T(8,128)S(1)} %get-tuple-element.35), channel_id=1, source_target_pairs={{1,0},{2,1},{3,2},{4,3},{5,4},{6,5},{7,6},{8,7},{9,8},{10,9},{11,1... | collective-permute-start | bytes 1572872 | tf_op jit(solution)/shard_map/ppermute | solution.py:26
  570.0 26.3 %collective-permute-start.31 = (f32[1,1,256,512]{3,2,1,0:T(8,128)S(1)}, f32[1,1,256,512]{3,2,1,0:T(8,128)S(1)}, u32[]{:S(2)}, u32[]{:S(2)}) collective-permute-start(f32[1,1,256,512]{3,2,1,0:T(8,128)S(1)} %get-tuple-element.42), channel_id=1, source_target_pairs={{0,1},{1,2},{2,3},{3,4},{4,5},{5,6},{6,7},{7,8},{8,9},{9,10},{10,1... | collective-permute-start | bytes 1572872 | tf_op jit(solution)/shard_map/ppermute | solution.py:23
  573.6 23.3 %collective-permute-start.30 = (f32[1,1,256,512]{3,2,1,0:T(8,128)S(1)}, f32[1,1,256,512]{3,2,1,0:T(8,128)S(1)}, u32[]{:S(2)}, u32[]{:S(2)}) collective-permute-start(f32[1,1,256,512]{3,2,1,0:T(8,128)S(1)} %get-tuple-element.43), channel_id=1, source_target_pairs={{1,0},{2,1},{3,2},{4,3},{5,4},{6,5},{7,6},{8,7},{9,8},{10,9},{11,1... | collective-permute-start | bytes 1572872 | tf_op jit(solution)/shard_map/ppermute | solution.py:26
  578.2 64.2 %collective-permute-start.24 = (f32[1,4,256,512]{3,2,1,0:T(8,128)}, f32[1,4,256,512]{3,2,1,0:T(8,128)}, u32[]{:S(2)}, u32[]{:S(2)}) collective-permute-start(f32[1,4,256,512]{3,2,1,0:T(8,128)} %multiply_add_fusion.1), channel_id=1, source_target_pairs={{0,16},{16,0},{1,17},{17,1},{2,18},{18,2},{3,19},{19,3},{4,20},{20... | collective-permute-start | bytes 6291464 | tf_op jit(solution)/shard_map/ppermute | solution.py:34
  642.4 10.6 %collective-permute-start.33 = (f32[1,4,256,512]{3,2,1,0:T(8,128)}, f32[1,4,256,512]{3,2,1,0:T(8,128)}, u32[]{:S(2)}, u32[]{:S(2)}) collective-permute-start(f32[1,4,256,512]{3,2,1,0:T(8,128)} %multiply_subtract_fusion), channel_id=1, source_target_pairs={{0,16},{16,0},{1,17},{17,1},{2,18},{18,2},{3,19},{19,3},{4,20},{20... | collective-permute-start | bytes 6291464 | tf_op jit(solution)/shard_map/ppermute | solution.py:34
  644.4 59.8 %collective-permute-start.32 = (f32[1,4,256,512]{3,2,1,0:T(8,128)}, f32[1,4,256,512]{3,2,1,0:T(8,128)}, u32[]{:S(2)}, u32[]{:S(2)}) collective-permute-start(f32[1,4,256,512]{3,2,1,0:T(8,128)} %multiply_add_fusion), channel_id=1, source_target_pairs={{0,16},{16,0},{1,17},{17,1},{2,18},{18,2},{3,19},{19,3},{4,20},{20... | collective-permute-start | bytes 6291464 | tf_op jit(solution)/shard_map/ppermute | solution.py:34
  (20 other events, 160.1 us)
where the time goes:
time: 718 us; the launch traced here: 708 us
  waiting for transfers between devices  272 us (38%)
  blocking collectives  186 us (26%)
  other arithmetic  150 us (21%)
  starting transfers between devices  85.5 us (12%)
    ppermute x13, waiting for transfers between devices, extended_2(): lax.ppermute(lax.slice_in_dim(block, block.shape[dim] - width, None, axis...  257 us
    psum x4, blocking collectives, colour_step(): upper, lower = lax.psum((upper_part, lower_part), 'sub')  139 us
    mul x28, other arithmetic, jacobi(): found = (found + scale * (resid - (6.0 + diag) * found + beside)) * mask  69 us
    psum x1, blocking collectives, shards(): lax.psum(jnp.sum(residual * residual, axis=(1, 2, 3)), ('colour', 'sub'))  47 us
    ppermute x13, starting transfers between devices, extended_2(): lax.ppermute(lax.slice_in_dim(block, block.shape[dim] - width, None, axis...  41.8 us
    ppermute x13, starting transfers between devices, extended_2(): lax.ppermute(lax.slice_in_dim(block, 0, width, axis=dim), axis, backward)  38.9 us
    sub x4, other arithmetic, colour_step(): return (current + alpha * correction, resid - alpha * image)  16.8 us
    reduce_sum x4, other arithmetic, colour_step(): lower_part = jnp.sum(correction * image, axis=(1, 2, 3))  14.4 us
  transfers between devices with their start and end apart: 34, of which 22 were waited for; matrix products, arithmetic and copies ran while one was open for 7% of the time, Pallas kernels for 0%

commit v1 on v0

v1 whole, which is shorter than its diff:
```python
import functools

import jax
import jax.numpy as jnp
from jax import lax
from jax.experimental import pallas as pl
from jax.experimental.pallas import tpu as pltpu
from jax.sharding import PartitionSpec as P

SWEEPS = 8
OMEGA = 0.8
RIM = 2 * SWEEPS
ROWS = 8
LANES = 128


def shift(value, last, axis, step):
    size = value.shape[axis]
    at = lax.broadcasted_iota(jnp.int32, value.shape, axis)
    if step > 0:
        return pltpu.roll(jnp.where(at == size - 1, last, value), 1, axis)
    return pltpu.roll(jnp.where(at == 0, last, value), size - 1, axis)


def lateral(planes, p, t, before, after):
    row = planes[p]
    zero = jnp.zeros_like(row[t])
    low = row[t - 1] if t > 0 else zero
    high = row[t + 1] if t + 1 < len(row) else zero
    total = shift(row[t], before, 0, 1) + shift(row[t], after, 0, -1)
    return total + (shift(row[t], low, 1, 1) + shift(row[t], high, 1, -1))


def lane(t):
    return slice(t * LANES, (t + 1) * LANES)


def solve_kernel(order, extra_ref, resid_ref, scale_ref, lo_ref, hi_ref, sq, ea, eb):
    _, rows, depth = scale_ref.shape
    tiles = depth // LANES
    span = len(order)
    refs = [(extra_ref, 0) if at < 0 else (resid_ref, at) for at in order]
    blank = jnp.zeros((span, ROWS, depth), jnp.float32)
    for buf in (ea, eb):
        buf[:, :ROWS, :] = blank
        buf[:, rows + ROWS :, :] = blank

    def first(j, carry):
        r = pl.multiple_of(j * ROWS, ROWS)
        for p, (ref, at) in enumerate(refs):
            value = scale_ref[p, pl.ds(r, ROWS), :] * ref[at, pl.ds(r, ROWS), :]
            sq[p, pl.ds(r, ROWS), :] = value
            ea[p, pl.ds(r + ROWS, ROWS), :] = value
        return carry

    lax.fori_loop(0, rows // ROWS, first, 0)
    src, dst = ea, eb
    for sweep in range(1, SWEEPS):
        final = sweep == SWEEPS - 1

        def body(j, carry, src=src, dst=dst, final=final):
            r = pl.multiple_of(j * ROWS, ROWS)
            planes = [
                [src[p, pl.ds(r + ROWS, ROWS), lane(t)] for t in range(tiles)] for p in range(span)
            ]
            for p in range(span):
                for t in range(tiles):
                    beside = lateral(
                        planes,
                        p,
                        t,
                        src[p, pl.ds(r, ROWS), lane(t)],
                        src[p, pl.ds(r + 2 * ROWS, ROWS), lane(t)],
                    )
                    if p > 0:
                        beside = beside + planes[p - 1][t]
                    if p + 1 < span:
                        beside = beside + planes[p + 1][t]
                    here = pl.ds(r, ROWS)
                    value = (1.0 - OMEGA) * planes[p][t] + sq[p, here, lane(t)]
                    value = value + scale_ref[p, here, lane(t)] * beside
                    if not final:
                        dst[p, pl.ds(r + ROWS, ROWS), lane(t)] = value
                    elif p < span // 2:
                        lo_ref[p, here, lane(t)] = value
                    else:
                        hi_ref[p - span // 2, here, lane(t)] = value
            return carry

        lax.fori_loop(0, rows // ROWS, body, 0)
        src, dst = dst, src


def solve(order, extra, resid, scale):
    span, rows, depth = scale.shape
    half = jax.ShapeDtypeStruct((span // 2, rows, depth), jnp.float32)
    padded = pltpu.VMEM((span, rows + 2 * ROWS, depth), jnp.float32)
    return pl.pallas_call(
        functools.partial(solve_kernel, order),
        out_shape=(half, half),
        in_specs=[pl.BlockSpec(memory_space=pltpu.VMEM)] * 3,
        out_specs=(pl.BlockSpec(memory_space=pltpu.VMEM),) * 2,
        scratch_shapes=[pltpu.VMEM((span, rows, depth), jnp.float32), padded, padded],
        compiler_params=pltpu.CompilerParams(vmem_limit_bytes=24 << 20),
        cost_estimate=pl.CostEstimate(
            flops=SWEEPS * 40 * span * rows * depth,
            bytes_accessed=20 * span * rows * depth,
            transcendentals=0,
        ),
        name="solve",
    )(extra, resid, scale)


def image_kernel(order, part_0, part_1, part_2, diag_ref, resid_ref, image_ref, dots_ref):
    count, rows, depth = diag_ref.shape
    tiles = depth // LANES
    parts = (part_0, part_1, part_2)
    rim = RIM // ROWS
    start = lax.axis_index("colour") * rim
    steps = rows // ROWS

    def body(j, carry):
        upper, lower = carry
        r = pl.multiple_of(j * ROWS, ROWS)
        below = pl.multiple_of(jnp.maximum(j - 1, 0) * ROWS, ROWS)
        above = pl.multiple_of(jnp.minimum(j + 1, steps - 1) * ROWS, ROWS)
        has_below = (j > 0).astype(jnp.float32)
        has_above = (j + 1 < steps).astype(jnp.float32)
        own = ((j >= start) & (j < start + steps - rim)).astype(jnp.float32)
        here = pl.ds(r, ROWS)
        planes = [[parts[k][at, here, lane(t)] for t in range(tiles)] for k, at in order]
        for p in range(count):
            k, at = order[p + 1]
            for t in range(tiles):
                before = parts[k][at, pl.ds(below, ROWS), lane(t)] * has_below
                after = parts[k][at, pl.ds(above, ROWS), lane(t)] * has_above
                beside = lateral(planes, p + 1, t, before, after)
                beside = beside + planes[p][t] + planes[p + 2][t]
                centre = planes[p + 1][t]
                value = (6.0 + diag_ref[p, here, lane(t)]) * centre - beside
                image_ref[p, here, lane(t)] = value
                weighted = centre * own
                upper = upper + resid_ref[p, here, lane(t)] * weighted
                lower = lower + weighted * value
        return upper, lower

    zero = jnp.zeros((ROWS, LANES), jnp.float32)
    upper, lower = lax.fori_loop(0, steps, body, (zero, zero))
    at = lax.broadcasted_iota(jnp.int32, (ROWS, LANES), 0)
    dots_ref[...] = jnp.where(at == 0, jnp.sum(upper), jnp.sum(lower))


def image_of(order, parts, diag, resid):
    count, rows, depth = diag.shape
    return pl.pallas_call(
        functools.partial(image_kernel, order),
        out_shape=(
            jax.ShapeDtypeStruct((count, rows, depth), jnp.float32),
            jax.ShapeDtypeStruct((ROWS, LANES), jnp.float32),
        ),
        in_specs=[pl.BlockSpec(memory_space=pltpu.VMEM)] * 5,
        out_specs=(pl.BlockSpec(memory_space=pltpu.VMEM),) * 2,
        compiler_params=pltpu.CompilerParams(vmem_limit_bytes=16 << 20),
        cost_estimate=pl.CostEstimate(
            flops=80 * count * rows * depth,
            bytes_accessed=20 * count * rows * depth,
            transcendentals=0,
        ),
        name="image",
    )(*parts, diag, resid)


def alpha_of(dots_ref):
    return jnp.broadcast_to(dots_ref[0:1, :] / dots_ref[1:2, :], (ROWS, LANES))


def update_kernel(dots_ref, resid_ref, image_ref, first_ref, out_ref):
    count, rows, depth = resid_ref.shape
    alpha = alpha_of(dots_ref)

    def body(j, carry):
        here = pl.ds(pl.multiple_of(j * ROWS, ROWS), ROWS)
        for p in range(count):
            for t in range(depth // LANES):
                value = resid_ref[p, here, lane(t)] - alpha * image_ref[p, here, lane(t)]
                out_ref[p, here, lane(t)] = value
                if p == 0:
                    first_ref[0, here, lane(t)] = value
        return carry

    lax.fori_loop(0, rows // ROWS, body, 0)


def update(dots, resid, image):
    count, rows, depth = resid.shape
    return pl.pallas_call(
        update_kernel,
        out_shape=(
            jax.ShapeDtypeStruct((1, rows, depth), jnp.float32),
            jax.ShapeDtypeStruct(resid.shape, jnp.float32),
        ),
        in_specs=[pl.BlockSpec(memory_space=pltpu.VMEM)] * 3,
        out_specs=(pl.BlockSpec(memory_space=pltpu.VMEM),) * 2,
        compiler_params=pltpu.CompilerParams(vmem_limit_bytes=16 << 20),
        cost_estimate=pl.CostEstimate(
            flops=4 * count * rows * depth,
            bytes_accessed=12 * count * rows * depth,
            transcendentals=0,
        ),
        name="update",
    )(dots, resid, image)


def finish_kernel(
    order_0, order_1, dots_0, dots_1, a_0, a_1, a_2, b_0, b_1, b_2, resid_ref, image_ref,
    kept_ref, sent_ref, norm_ref,
):
    count, rows, depth = resid_ref.shape
    half = depth // 2
    me = lax.axis_index("colour")
    alpha_0 = alpha_of(dots_0)
    alpha_1 = alpha_of(dots_1)
    first, second = (a_0, a_1, a_2), (b_0, b_1, b_2)

    def body(j, acc):
        here = pl.ds(pl.multiple_of(me * RIM + j * ROWS, ROWS), ROWS)
        there = pl.ds(pl.multiple_of(j * ROWS, ROWS), ROWS)
        for out, side in ((kept_ref, me), (sent_ref, 1 - me)):
            for t in range(half // LANES):
                at_z = pl.ds(pl.multiple_of(side * half + t * LANES, LANES), LANES)
                for p in range(count):
                    k, at = order_0[p + 1]
                    m, to = order_1[p + 1]
                    u = alpha_0 * first[k][at, here, at_z] + alpha_1 * second[m][to, here, at_z]
                    q = resid_ref[p, here, at_z] - alpha_1 * image_ref[p, here, at_z]
                    out[0, p, there, lane(t)] = u
                    out[1, p, there, lane(t)] = q
                    acc = acc + q * q
        return acc

    steps = kept_ref.shape[2] // ROWS
    acc = lax.fori_loop(0, steps, body, jnp.zeros((ROWS, LANES), jnp.float32))
    norm_ref[...] = jnp.broadcast_to(jnp.sum(acc), (ROWS, LANES))


def finish(order_0, order_1, dots_0, dots_1, parts_0, parts_1, resid, image):
    count, rows, depth = resid.shape
    block = jax.ShapeDtypeStruct((2, count, rows - RIM, depth // 2), jnp.float32)
    return pl.pallas_call(
        functools.partial(finish_kernel, order_0, order_1),
        out_shape=(block, block, jax.ShapeDtypeStruct((ROWS, LANES), jnp.float32)),
        in_specs=[pl.BlockSpec(memory_space=pltpu.VMEM)] * 10,
        out_specs=(pl.BlockSpec(memory_space=pltpu.VMEM),) * 3,
        compiler_params=pltpu.CompilerParams(vmem_limit_bytes=24 << 20),
        cost_estimate=pl.CostEstimate(
            flops=8 * count * rows * depth,
            bytes_accessed=24 * count * rows * depth,
            transcendentals=0,
        ),
        name="finish",
    )(dots_0, dots_1, *parts_0, *parts_1, resid, image)


ORDER_0 = ((0, 0), (0, 1), (1, 0), (1, 1), (2, 0), (2, 1))
ORDER_1 = ((2, 0), (2, 1), (0, 0), (0, 1), (1, 0), (1, 1))


def shards(rhs, diagonal):
    colour = lax.axis_index("colour")
    device = lax.axis_index("sub")
    count = lax.axis_size("sub")
    nrhs, _, ny, _ = rhs.shape
    rows = ny // 2 + RIM
    begin = colour * (ny // 2 - RIM)
    to_right = [(i, i + 1) for i in range(count - 1)]
    to_left = [(i + 1, i) for i in range(count - 1)]

    source = lax.dynamic_slice_in_dim(rhs, begin, rows, 2)
    diag = lax.dynamic_slice_in_dim(diagonal, begin, rows, 1)
    diag_low = lax.ppermute(diag[-1:], "sub", to_right)
    low = [lax.ppermute(source[n, -1:], "sub", to_right) for n in range(nrhs)]
    diag_high = lax.ppermute(diag[:1], "sub", to_left)
    has_low = (device > 0).astype(jnp.float32)
    has_high = (device < count - 1).astype(jnp.float32)
    scale = OMEGA / (6.0 + diag)
    scale_0 = jnp.concatenate([has_low * (OMEGA / (6.0 + diag_low)), scale[:-1]], axis=0)
    scale_1 = jnp.concatenate([scale[1:], has_high * (OMEGA / (6.0 + diag_high))], axis=0)

    q = [source[n] for n in range(nrhs)]
    parts_0, parts_1, dots_0, dots_1 = [], [], [], []
    images, q1, high = [], [], []
    for n in range(nrhs):
        lo, hi = solve((-1, 0, 1, 2), low[n], q[n], scale_0)
        parts_0.append((lo, hi, lax.ppermute(lo, "sub", to_left)))
    for n in range(nrhs):
        image, dots = image_of(ORDER_0, parts_0[n], diag, q[n])
        images.append(image)
        dots_0.append(lax.psum(dots, ("colour", "sub")))
    for n in range(nrhs):
        edge, resid = update(dots_0[n], q[n], images[n])
        q1.append(resid)
        high.append(lax.ppermute(edge, "sub", to_left))
    for n in range(nrhs):
        lo, hi = solve((1, 2, 3, -1), high[n], q1[n], scale_1)
        parts_1.append((lo, hi, lax.ppermute(hi, "sub", to_right)))
    images = []
    for n in range(nrhs):
        image, dots = image_of(ORDER_1, parts_1[n], diag, q1[n])
        images.append(image)
        dots_1.append(lax.psum(dots, ("colour", "sub")))
    outs, norms = [], []
    for n in range(nrhs):
        kept, sent, norm = finish(
            ORDER_0, ORDER_1, dots_0[n], dots_1[n], parts_0[n], parts_1[n], q1[n], images[n]
        )
        got = lax.ppermute(sent, "colour", [(0, 1), (1, 0)])
        first = colour == 0
        below = jnp.where(first, kept, got)
        above = jnp.where(first, got, kept)
        outs.append(jnp.concatenate([below, above], axis=2))
        norms.append(norm[0, 0])
    solution = jnp.stack([out[0] for out in outs])
    residual = jnp.stack([out[1] for out in outs])
    squares = lax.psum(jnp.stack(norms), ("colour", "sub"))
    return solution, residual, jnp.sqrt(squares)


def solution(mesh):
    placed = (P(None, "sub", None, None), P("sub", None, None))
    return jax.shard_map(
        shards,
        mesh=mesh,
        in_specs=placed,
        out_specs=(P(None, "sub", None, "colour"), P(None, "sub", None, "colour"), P()),
        check_vma=False,
    )
```

time: 718 us -> 351 us (0.49); the launches traced: 708 us -> 348 us
  waiting for transfers between devices: 272 us -> 20.7 us
  other arithmetic: 150 us -> 12.6 us
  Pallas kernels: 0 us -> 113 us
  blocking collectives: 186 us -> 121 us
  starting transfers between devices: 85.5 us -> 46.6 us
  local copies, waits for them, and re-layouts: 7.01 us -> 32.2 us
    ppermute x34 -> x17, waiting for transfers between devices: 272 us -> 20.7 us  [the longest x3 7.13 us: shards(): high.append(lax.ppermute(edge, 'sub', to_left))]
    pallas_call x0 -> x18, Pallas kernels: none -> 113 us  [the longest x6 87.2 us: solve(): pl.pallas_call(functools.partial(solve_kernel, order), out_shape=(half, h...]
    mul x29 -> x2, other arithmetic: 70.7 us -> 2.12 us  [the longest x1 1.11 us: shards(): has_low * (OMEGA / (6.0 + diag_low))]
    psum x5 -> x3, blocking collectives: 186 us -> 121 us  [the longest x1 40.6 us: shards(): dots_1.append(lax.psum(dots, ('colour', 'sub')))]
    ppermute x34 -> x17, starting transfers between devices: 85.5 us -> 46.6 us  [the longest x3 10.5 us: shards(): high.append(lax.ppermute(edge, 'sub', to_left))]
    unnamed x68 -> x112, local copies, waits for them, and re-layouts: 2.59 us -> 20 us
    sub x4 -> x0, other arithmetic: 16.8 us -> none  [colour_step(): return (current + alpha * correction, resid - alpha * image)]
    reduce_sum x5 -> x0, other arithmetic: 16.4 us -> none  [the longest x4 14.4 us: colour_step(): lower_part = jnp.sum(correction * image, axis=(1, 2, 3))]
  transfers between devices with their start and end apart: 34 -> 17, of which waited for: 22 -> 4; matrix products, arithmetic and copies ran while one was open for 7% -> 5% of each run, Pallas kernels for 0% -> 31%
where the time goes in v1:
time: 351 us; the launch traced here: 348 us
  blocking collectives  121 us (34%)
  Pallas kernels  113 us (32%)
  starting transfers between devices  46.6 us (13%)
  local copies, waits for them, and re-layouts  32.2 us (9%)
  waiting for transfers between devices  20.7 us (6%)
  other arithmetic  12.6 us (4%)
    pallas_call x6, Pallas kernels, solve(): pl.pallas_call(functools.partial(solve_kernel, order), out_shape=(half, h...  87.2 us
    psum x1, blocking collectives, shards(): dots_1.append(lax.psum(dots, ('colour', 'sub')))  40.6 us
    psum x1, blocking collectives, shards(): dots_0.append(lax.psum(dots, ('colour', 'sub')))  40.5 us
    psum x1, blocking collectives, shards(): squares = lax.psum(jnp.stack(norms), ('colour', 'sub'))  40.4 us
    unnamed x112, local copies, waits for them, and re-layouts  20 us
    pallas_call x6, Pallas kernels, image_of(): pl.pallas_call(functools.partial(image_kernel, order), out_shape=(jax.Sha...  16.5 us
    ppermute x3, starting transfers between devices, shards(): high.append(lax.ppermute(edge, 'sub', to_left))  10.5 us
    ppermute x3, starting transfers between devices, shards(): low = [lax.ppermute(source[n, -1:], 'sub', to_right) for n in range(nrhs)]  10.3 us
  transfers between devices with their start and end apart: 17, of which 4 were waited for; matrix products, arithmetic and copies ran while one was open for 5% of the time, Pallas kernels for 31%

profile of v1, /device:TPU:10, one launch (start us, length us, event | category | flops | bytes accessed | tf_op | source)
XLA Modules:
  0.0 348.4 jit_solution(13762836463962066879)
XLA Ops:
  0.6 1.9 constant_dynamic-slice_fusion
  2.6 3.4 collective-permute-start.1
  5.9 2.1 dynamic-slice_bitcast_fusion.5
  8.0 3.4 collective-permute-start
  11.4 3.4 collective-permute-start.12
  14.9 3.5 %collective-permute-start.7 = (f32[1,144,512]{2,1,0:T(8,128)}, f32[1,144,512]{2,1,0:T(8,128)}, u32[]{:S(2)}, u32[]{:S(2)}) collective-permute-start(f32[1,144,512]{2,1,0:T(8,128)} %get-tuple-element.94), channel_id=1, source_target_pairs={{0,1},{1,2},{2,3},{3,4},{4,5},{5,6},{6,7},{7,8},{8,9},{9,10},{10,1... | collective-permute-start | bytes 884744 | tf_op jit(solution)/shard_map/ppermute | solution.py:281
  18.4 3.6 %dynamic-slice_bitcast_fusion.2 = (f32[4,144,512]{2,1,0:T(8,128)S(1)}, f32[4,144,512]{2,1,0:T(8,128)}, f32[4,144,512]{2,1,0:T(8,128)S(1)}) fusion(f32[3,4,256,512]{3,2,1,0:T(8,128)} %param.2, s32[]{:T(128)S(6)} %select_n.33, s32[]{:T(128)S(6)} %add.37, s32[]{:T(128)S(6)} %add.40), kind=kLoop, calls=%fused_computation.18 | loop fusion | bytes 7077900 | tf_op jit(solution)/shard_map/squeeze | solution.py:289
  23.2 2.6 fusion.6
  27.0 5.4 %collective-permute-done.7.extra_ref = f32[1,144,512]{2,1,0:T(8,128)} collective-permute-done((f32[1,144,512]{2,1,0:T(8,128)}, f32[1,144,512]{2,1,0:T(8,128)}, u32[]{:S(2)}, u32[]{:S(2)}) %collective-permute-start.7) | collective-permute-done | bytes 294944 | tf_op jit(solution)/shard_map/ppermute | solution.py:281
  32.5 15.5 %solve.8 = (f32[2,144,512]{2,1,0:T(8,128)}, f32[2,144,512]{2,1,0:T(8,128)S(1)}) custom-call(f32[1,144,512]{2,1,0:T(8,128)} %collective-permute-done.7.extra_ref, f32[4,144,512]{2,1,0:T(8,128)S(1)} %copy-done, f32[4,144,512]{2,1,0:T(8,128)S(1)} %pad_maximum_fusion.2.scale_ref), custom_call_target="tpu_custom_call" | custom-call | flops 94371840 | bytes 5898240 | tf_op jit(solution)/shard_map/solve/pallas_call | solution.py:98
  48.8 4.2 %collective-permute-start.8 = (f32[2,144,512]{2,1,0:T(8,128)}, f32[2,144,512]{2,1,0:T(8,128)}, u32[]{:S(2)}, u32[]{:S(2)}) collective-permute-start(f32[2,144,512]{2,1,0:T(8,128)} %get-tuple-element.54.part_0.a_0), channel_id=1, source_target_pairs={{1,0},{2,1},{3,2},{4,3},{5,4},{6,5},{7,6},{8,7},{9,8},{10,9},{11,1... | collective-permute-start | bytes 1769480 | tf_op jit(solution)/shard_map/ppermute | solution.py:294
  53.0 15.4 %solve.10 = (f32[2,144,512]{2,1,0:T(8,128)}, f32[2,144,512]{2,1,0:T(8,128)S(1)}) custom-call(f32[1,144,512]{2,1,0:T(8,128)} %collective-permute-done.12.extra_ref, f32[4,144,512]{2,1,0:T(8,128)S(1)} %get-tuple-element.91.resid_ref, f32[4,144,512]{2,1,0:T(8,128)S(1)} %pad_maximum_fusion.2.scale_ref), custom_call_target="tpu_custom_call" | custom-call | flops 94371840 | bytes 5898240 | tf_op jit(solution)/shard_map/solve/pallas_call | solution.py:98
  69.2 2.4 collective-permute-start.13
  71.7 15.4 %solve.6 = (f32[2,144,512]{2,1,0:T(8,128)}, f32[2,144,512]{2,1,0:T(8,128)S(1)}) custom-call(f32[1,144,512]{2,1,0:T(8,128)} %collective-permute-done.extra_ref, f32[4,144,512]{2,1,0:T(8,128)S(1)} %get-tuple-element.89.resid_ref, f32[4,144,512]{2,1,0:T(8,128)S(1)} %pad_maximum_fusion.2.scale_ref), custom_call_target="tpu_custom_call" | custom-call | flops 94371840 | bytes 5898240 | tf_op jit(solution)/shard_map/solve/pallas_call | solution.py:98
  88.0 3.3 collective-permute-start.2
  91.3 2.4 collective-permute-start.4
  95.0 3.4 image.10
  99.4 3.4 image.8
  102.8 4.5 %collective-permute-done.2.part_2.a_2 = f32[2,144,512]{2,1,0:T(8,128)} collective-permute-done((f32[2,144,512]{2,1,0:T(8,128)}, f32[2,144,512]{2,1,0:T(8,128)}, u32[]{:S(2)}, u32[]{:S(2)}) %collective-permute-start.2) | collective-permute-done | bytes 589856 | tf_op jit(solution)/shard_map/ppermute | solution.py:294
  107.3 3.3 image.6
  112.3 40.5 %all-reduce.1 = (f32[8,128]{1,0:T(8,128)S(1)}, f32[8,128]{1,0:T(8,128)S(1)}, f32[8,128]{1,0:T(8,128)S(1)}) all-reduce(f32[8,128]{1,0:T(8,128)S(1)} %get-tuple-element.68, f32[8,128]{1,0:T(8,128)} %copy-done.49, f32[8,128]{1,0:T(8,128)} %copy-done.51), channel_id=1, replica_groups=mesh['colour'=2,'sub'=16] {'colour','sub'}, use_global_device_ids=true, to_apply=%region_4.0 | all-reduce | flops 3072 | bytes 24576 | tf_op jit(solution)/shard_map/psum | solution.py:298
  152.8 1.3 copy-done.2
  154.0 1.3 copy-done.39
  155.5 2.2 collective-permute-start.9
  158.0 5.0 %collective-permute-start.14 = (f32[1,144,512]{2,1,0:T(8,128)S(1)}, f32[1,144,512]{2,1,0:T(8,128)S(1)}, u32[]{:S(2)}, u32[]{:S(2)}) collective-permute-start(f32[1,144,512]{2,1,0:T(8,128)S(1)} %get-tuple-element.70), channel_id=1, source_target_pairs={{1,0},{2,1},{3,2},{4,3},{5,4},{6,5},{7,6},{8,7},{9,8},{10,9},{11,1... | collective-permute-start | bytes 884744 | tf_op jit(solution)/shard_map/ppermute | solution.py:302
  163.2 3.3 collective-permute-start.3
  167.7 7.1 %collective-permute-done.14.extra_ref = f32[1,144,512]{2,1,0:T(8,128)S(1)} collective-permute-done((f32[1,144,512]{2,1,0:T(8,128)S(1)}, f32[1,144,512]{2,1,0:T(8,128)S(1)}, u32[]{:S(2)}, u32[]{:S(2)}) %collective-permute-start.14) | collective-permute-done | bytes 294944 | tf_op jit(solution)/shard_map/ppermute | solution.py:302
  174.8 13.6 %solve.11 = (f32[2,144,512]{2,1,0:T(8,128)S(1)}, f32[2,144,512]{2,1,0:T(8,128)S(1)}) custom-call(f32[1,144,512]{2,1,0:T(8,128)S(1)} %collective-permute-done.14.extra_ref, f32[4,144,512]{2,1,0:T(8,128)S(1)} %get-tuple-element.71.resid_ref, f32[4,144,512]{2,1,0:T(8,128)S(1)} %pad_maximum_fusion.3.scale_ref), custom_call_target="tpu_custom_call" | custom-call | flops 94371840 | bytes 5898240 | tf_op jit(solution)/shard_map/solve/pallas_call | solution.py:98
  188.4 2.5 collective-permute-start.15
  191.0 13.6 %solve.9 = (f32[2,144,512]{2,1,0:T(8,128)S(1)}, f32[2,144,512]{2,1,0:T(8,128)S(1)}) custom-call(f32[1,144,512]{2,1,0:T(8,128)S(1)} %collective-permute-done.9.extra_ref, f32[4,144,512]{2,1,0:T(8,128)S(1)} %get-tuple-element.59.resid_ref, f32[4,144,512]{2,1,0:T(8,128)S(1)} %pad_maximum_fusion.3.scale_ref), custom_call_target="tpu_custom_call" | custom-call | flops 94371840 | bytes 5898240 | tf_op jit(solution)/shard_map/solve/pallas_call | solution.py:98
  204.6 5.1 %collective-permute-start.10 = (f32[2,144,512]{2,1,0:T(8,128)S(1)}, f32[2,144,512]{2,1,0:T(8,128)S(1)}, u32[]{:S(2)}, u32[]{:S(2)}) collective-permute-start(f32[2,144,512]{2,1,0:T(8,128)S(1)} %get-tuple-element.61.part_1.b_1), channel_id=1, source_target_pairs={{0,1},{1,2},{2,3},{3,4},{4,5},{5,6},{6,7},{7,8},{8,9},{9,10},{10,1... | collective-permute-start | bytes 1769480 | tf_op jit(solution)/shard_map/ppermute | solution.py:305
  209.7 13.6 %solve.7 = (f32[2,144,512]{2,1,0:T(8,128)S(1)}, f32[2,144,512]{2,1,0:T(8,128)S(1)}) custom-call(f32[1,144,512]{2,1,0:T(8,128)S(1)} %collective-permute-done.3.extra_ref, f32[4,144,512]{2,1,0:T(8,128)S(1)} %get-tuple-element.47.resid_ref, f32[4,144,512]{2,1,0:T(8,128)S(1)} %pad_maximum_fusion.3.scale_ref), custom_call_target="tpu_custom_call" | custom-call | flops 94371840 | bytes 5898240 | tf_op jit(solution)/shard_map/solve/pallas_call | solution.py:98
  223.3 1.9 collective-permute-start.5
  225.3 2.1 image.9
  227.5 2.1 image.11
  231.4 3.7 %collective-permute-done.5.part_2.b_2 = f32[2,144,512]{2,1,0:T(8,128)S(1)} collective-permute-done((f32[2,144,512]{2,1,0:T(8,128)S(1)}, f32[2,144,512]{2,1,0:T(8,128)S(1)}, u32[]{:S(2)}, u32[]{:S(2)}) %collective-permute-start.5) | collective-permute-done | bytes 589856 | tf_op jit(solution)/shard_map/ppermute | solution.py:305
  235.1 2.1 image.7
  238.9 40.6 %all-reduce = (f32[8,128]{1,0:T(8,128)}, f32[8,128]{1,0:T(8,128)S(1)}, f32[8,128]{1,0:T(8,128)}) all-reduce(f32[8,128]{1,0:T(8,128)} %copy-done.48, f32[8,128]{1,0:T(8,128)S(1)} %get-tuple-element.62, f32[8,128]{1,0:T(8,128)} %copy-done.50), channel_id=1, replica_groups=mesh['colour'=2,'sub'=16] {'colour','sub'}, use_global_device_ids=true, to_apply=%region_5.0 | all-reduce | flops 3072 | bytes 24576 | tf_op jit(solution)/shard_map/psum | solution.py:310
  283.7 1.3 copy-done.45
  285.0 3.1 finish.4
  288.2 3.0 finish.5
  291.8 2.9 finish.3
  297.2 1.9 pad_maximum_fusion.4
  299.1 40.4 %psum.55 = f32[3]{0:T(128)S(1)} all-reduce(f32[3]{0:T(128)S(1)} %pad_maximum_fusion.4), channel_id=1, replica_groups=mesh['colour'=2,'sub'=16] {'colour','sub'}, use_global_device_ids=true, to_apply=%region_6.7 | all-reduce | flops 3 | bytes 24 | tf_op jit(solution)/shard_map/psum | solution.py:324
  340.0 1.4 broadcast_select_fusion.2
  341.5 1.4 broadcast_select_fusion
  344.4 1.9 fusion
  346.3 2.1 pad_maximum_fusion.1
  (141 shorter events, 23.4 us)
Async XLA Ops:
  2.6 23.3 %collective-permute-start.1 = (f32[1,144,512]{2,1,0:T(8,128)}, f32[1,144,512]{2,1,0:T(8,128)}, u32[]{:S(2)}, u32[]{:S(2)}) collective-permute-start(f32[1,144,512]{2,1,0:T(8,128)} %get-tuple-element.102), channel_id=1, source_target_pairs={{0,1},{1,2},{2,3},{3,4},{4,5},{5,6},{6,7},{7,8},{8,9},{9,10},{10,1... | collective-permute-start | bytes 884744 | tf_op jit(solution)/shard_map/ppermute | solution.py:280
  8.0 63.6 %collective-permute-start = (f32[1,144,512]{2,1,0:T(8,128)}, f32[1,144,512]{2,1,0:T(8,128)}, u32[]{:S(2)}, u32[]{:S(2)}) collective-permute-start(f32[1,144,512]{2,1,0:T(8,128)} %get-tuple-element.92), channel_id=1, source_target_pairs={{0,1},{1,2},{2,3},{3,4},{4,5},{5,6},{6,7},{7,8},{8,9},{9,10},{10,1... | collective-permute-start | bytes 884744 | tf_op jit(solution)/shard_map/ppermute | solution.py:281
  11.4 41.6 %collective-permute-start.12 = (f32[1,144,512]{2,1,0:T(8,128)}, f32[1,144,512]{2,1,0:T(8,128)}, u32[]{:S(2)}, u32[]{:S(2)}) collective-permute-start(f32[1,144,512]{2,1,0:T(8,128)} %get-tuple-element.93), channel_id=1, source_target_pairs={{0,1},{1,2},{2,3},{3,4},{4,5},{5,6},{6,7},{7,8},{8,9},{9,10},{10,1... | collective-permute-start | bytes 884744 | tf_op jit(solution)/shard_map/ppermute | solution.py:281
  14.8 7.1 %copy-start.55 = (f32[4,256,512]{2,1,0:T(8,128)S(1)}, f32[4,256,512]{2,1,0:T(8,128)}, u32[]{:S(2)}) copy-start(f32[4,256,512]{2,1,0:T(8,128)} %param.3) | copy-start | bytes 6291460
  14.9 17.6 %collective-permute-start.7 = (f32[1,144,512]{2,1,0:T(8,128)}, f32[1,144,512]{2,1,0:T(8,128)}, u32[]{:S(2)}, u32[]{:S(2)}) collective-permute-start(f32[1,144,512]{2,1,0:T(8,128)} %get-tuple-element.94), channel_id=1, source_target_pairs={{0,1},{1,2},{2,3},{3,4},{4,5},{5,6},{6,7},{7,8},{8,9},{9,10},{10,1... | collective-permute-start | bytes 884744 | tf_op jit(solution)/shard_map/ppermute | solution.py:281
  25.8 6.6 %copy-start = (f32[4,144,512]{2,1,0:T(8,128)S(1)}, f32[4,144,512]{2,1,0:T(8,128)}, u32[]{:S(2)}) copy-start(f32[4,144,512]{2,1,0:T(8,128)} %get-tuple-element.90.resid_ref) | copy-start | bytes 3538948
  48.8 50.6 %collective-permute-start.8 = (f32[2,144,512]{2,1,0:T(8,128)}, f32[2,144,512]{2,1,0:T(8,128)}, u32[]{:S(2)}, u32[]{:S(2)}) collective-permute-start(f32[2,144,512]{2,1,0:T(8,128)} %get-tuple-element.54.part_0.a_0), channel_id=1, source_target_pairs={{1,0},{2,1},{3,2},{4,3},{5,4},{6,5},{7,6},{8,7},{9,8},{10,9},{11,1... | collective-permute-start | bytes 1769480 | tf_op jit(solution)/shard_map/ppermute | solution.py:294
  69.2 24.6 %collective-permute-start.13 = (f32[2,144,512]{2,1,0:T(8,128)}, f32[2,144,512]{2,1,0:T(8,128)}, u32[]{:S(2)}, u32[]{:S(2)}) collective-permute-start(f32[2,144,512]{2,1,0:T(8,128)} %get-tuple-element.66.part_0.a_0), channel_id=1, source_target_pairs={{1,0},{2,1},{3,2},{4,3},{5,4},{6,5},{7,6},{8,7},{9,8},{10,9},{11,1... | collective-permute-start | bytes 1769480 | tf_op jit(solution)/shard_map/ppermute | solution.py:294
  88.0 19.3 %collective-permute-start.2 = (f32[2,144,512]{2,1,0:T(8,128)}, f32[2,144,512]{2,1,0:T(8,128)}, u32[]{:S(2)}, u32[]{:S(2)}) collective-permute-start(f32[2,144,512]{2,1,0:T(8,128)} %get-tuple-element.42.part_0.a_0), channel_id=1, source_target_pairs={{1,0},{2,1},{3,2},{4,3},{5,4},{6,5},{7,6},{8,7},{9,8},{10,9},{11,1... | collective-permute-start | bytes 1769480 | tf_op jit(solution)/shard_map/ppermute | solution.py:294
  91.3 75.2 %collective-permute-start.4 = (f32[1,144,512]{2,1,0:T(8,128)}, f32[1,144,512]{2,1,0:T(8,128)}, u32[]{:S(2)}, u32[]{:S(2)}) collective-permute-start(f32[1,144,512]{2,1,0:T(8,128)} %get-tuple-element.101), channel_id=1, source_target_pairs={{1,0},{2,1},{3,2},{4,3},{5,4},{6,5},{7,6},{8,7},{9,8},{10,9},{11,1... | collective-permute-start | bytes 884744 | tf_op jit(solution)/shard_map/ppermute | solution.py:282
  93.8 5.6 %copy-start.1 = (f32[4,144,512]{2,1,0:T(8,128)S(1)}, f32[4,144,512]{2,1,0:T(8,128)}, u32[]{:S(2)}) copy-start(f32[4,144,512]{2,1,0:T(8,128)} %get-tuple-element.90.resid_ref) | copy-start | bytes 3538948
  95.0 4.4 %copy-start.14 = (f32[2,144,512]{2,1,0:T(8,128)S(1)}, f32[2,144,512]{2,1,0:T(8,128)}, u32[]{:S(2)}) copy-start(f32[2,144,512]{2,1,0:T(8,128)} %copy-done.13) | copy-start | bytes 1769476
  99.4 7.9 %copy-start.8 = (f32[2,144,512]{2,1,0:T(8,128)S(1)}, f32[2,144,512]{2,1,0:T(8,128)}, u32[]{:S(2)}) copy-start(f32[2,144,512]{2,1,0:T(8,128)} %copy-done.7) | copy-start | bytes 1769476
  102.8 7.8 %copy-start.38 = (f32[4,144,512]{2,1,0:T(8,128)}, f32[4,144,512]{2,1,0:T(8,128)S(1)}, u32[]{:S(2)}) copy-start(f32[4,144,512]{2,1,0:T(8,128)S(1)} %get-tuple-element.57.image_ref) | copy-start | bytes 3538948
  102.8 8.8 %copy-start.49 = (f32[8,128]{1,0:T(8,128)}, f32[8,128]{1,0:T(8,128)S(1)}, u32[]{:S(2)}) copy-start(f32[8,128]{1,0:T(8,128)S(1)} %get-tuple-element.56) | copy-start | bytes 12292
  155.3 7.7 %copy-start.37 = (f32[4,144,512]{2,1,0:T(8,128)S(1)}, f32[4,144,512]{2,1,0:T(8,128)}, u32[]{:S(2)}) copy-start(f32[4,144,512]{2,1,0:T(8,128)} %copy-done.36) | copy-start | bytes 3538948
  155.5 69.8 %copy-start.5 = (f32[4,144,512]{2,1,0:T(8,128)}, f32[4,144,512]{2,1,0:T(8,128)S(1)}, u32[]{:S(2)}) copy-start(f32[4,144,512]{2,1,0:T(8,128)S(1)} %get-tuple-element.59.resid_ref) | copy-start | bytes 3538948
  155.5 35.4 %collective-permute-start.9 = (f32[1,144,512]{2,1,0:T(8,128)S(1)}, f32[1,144,512]{2,1,0:T(8,128)S(1)}, u32[]{:S(2)}, u32[]{:S(2)}) collective-permute-start(f32[1,144,512]{2,1,0:T(8,128)S(1)} %get-tuple-element.58), channel_id=1, source_target_pairs={{1,0},{2,1},{3,2},{4,3},{5,4},{6,5},{7,6},{8,7},{9,8},{10,9},{11,1... | collective-permute-start | bytes 884744 | tf_op jit(solution)/shard_map/ppermute | solution.py:302
  157.7 9.8 %copy-start.54 = (f32[3,144,512]{2,1,0:T(8,128)S(1)}, f32[3,144,512]{2,1,0:T(8,128)}, u32[]{:S(2)}) copy-start(f32[3,144,512]{2,1,0:T(8,128)} %get-tuple-element.103) | copy-start | bytes 2654212
  158.0 69.5 %copy-start.3 = (f32[4,144,512]{2,1,0:T(8,128)}, f32[4,144,512]{2,1,0:T(8,128)S(1)}, u32[]{:S(2)}) copy-start(f32[4,144,512]{2,1,0:T(8,128)S(1)} %get-tuple-element.71.resid_ref) | copy-start | bytes 3538948
  158.0 16.8 %collective-permute-start.14 = (f32[1,144,512]{2,1,0:T(8,128)S(1)}, f32[1,144,512]{2,1,0:T(8,128)S(1)}, u32[]{:S(2)}, u32[]{:S(2)}) collective-permute-start(f32[1,144,512]{2,1,0:T(8,128)S(1)} %get-tuple-element.70), channel_id=1, source_target_pairs={{1,0},{2,1},{3,2},{4,3},{5,4},{6,5},{7,6},{8,7},{9,8},{10,9},{11,1... | collective-permute-start | bytes 884744 | tf_op jit(solution)/shard_map/ppermute | solution.py:302
  163.2 46.5 %collective-permute-start.3 = (f32[1,144,512]{2,1,0:T(8,128)S(1)}, f32[1,144,512]{2,1,0:T(8,128)S(1)}, u32[]{:S(2)}, u32[]{:S(2)}) collective-permute-start(f32[1,144,512]{2,1,0:T(8,128)S(1)} %get-tuple-element.46), channel_id=1, source_target_pairs={{1,0},{2,1},{3,2},{4,3},{5,4},{6,5},{7,6},{8,7},{9,8},{10,9},{11,1... | collective-permute-start | bytes 884744 | tf_op jit(solution)/shard_map/ppermute | solution.py:302
  188.4 39.0 %copy-start.16 = (f32[2,144,512]{2,1,0:T(8,128)}, f32[2,144,512]{2,1,0:T(8,128)S(1)}, u32[]{:S(2)}) copy-start(f32[2,144,512]{2,1,0:T(8,128)S(1)} %get-tuple-element.72.part_0.b_0) | copy-start | bytes 1769476
  188.4 39.0 %copy-start.18 = (f32[2,144,512]{2,1,0:T(8,128)}, f32[2,144,512]{2,1,0:T(8,128)S(1)}, u32[]{:S(2)}) copy-start(f32[2,144,512]{2,1,0:T(8,128)S(1)} %get-tuple-element.73.part_1.b_1) | copy-start | bytes 1769476
  188.4 39.0 %collective-permute-start.15 = (f32[2,144,512]{2,1,0:T(8,128)S(1)}, f32[2,144,512]{2,1,0:T(8,128)S(1)}, u32[]{:S(2)}, u32[]{:S(2)}) collective-permute-start(f32[2,144,512]{2,1,0:T(8,128)S(1)} %get-tuple-element.73.part_1.b_1), channel_id=1, source_target_pairs={{0,1},{1,2},{2,3},{3,4},{4,5},{5,6},{6,7},{7,8},{8,9},{9,10},{10,1... | collective-permute-start | bytes 1769480 | tf_op jit(solution)/shard_map/ppermute | solution.py:305
  204.6 22.8 %copy-start.28 = (f32[2,144,512]{2,1,0:T(8,128)}, f32[2,144,512]{2,1,0:T(8,128)S(1)}, u32[]{:S(2)}) copy-start(f32[2,144,512]{2,1,0:T(8,128)S(1)} %get-tuple-element.60.part_0.b_0) | copy-start | bytes 1769476
  204.6 22.8 %copy-start.30 = (f32[2,144,512]{2,1,0:T(8,128)}, f32[2,144,512]{2,1,0:T(8,128)S(1)}, u32[]{:S(2)}) copy-start(f32[2,144,512]{2,1,0:T(8,128)S(1)} %get-tuple-element.61.part_1.b_1) | copy-start | bytes 1769476
  204.6 20.7 %collective-permute-start.10 = (f32[2,144,512]{2,1,0:T(8,128)S(1)}, f32[2,144,512]{2,1,0:T(8,128)S(1)}, u32[]{:S(2)}, u32[]{:S(2)}) collective-permute-start(f32[2,144,512]{2,1,0:T(8,128)S(1)} %get-tuple-element.61.part_1.b_1), channel_id=1, source_target_pairs={{0,1},{1,2},{2,3},{3,4},{4,5},{5,6},{6,7},{7,8},{8,9},{9,10},{10,1... | collective-permute-start | bytes 1769480 | tf_op jit(solution)/shard_map/ppermute | solution.py:305
  223.3 11.8 %copy-start.22 = (f32[2,144,512]{2,1,0:T(8,128)}, f32[2,144,512]{2,1,0:T(8,128)S(1)}, u32[]{:S(2)}) copy-start(f32[2,144,512]{2,1,0:T(8,128)S(1)} %get-tuple-element.48.part_0.b_0) | copy-start | bytes 1769476
  223.3 11.8 %copy-start.24 = (f32[2,144,512]{2,1,0:T(8,128)}, f32[2,144,512]{2,1,0:T(8,128)S(1)}, u32[]{:S(2)}) copy-start(f32[2,144,512]{2,1,0:T(8,128)S(1)} %get-tuple-element.49.part_1.b_1) | copy-start | bytes 1769476
  223.3 11.8 %collective-permute-start.5 = (f32[2,144,512]{2,1,0:T(8,128)S(1)}, f32[2,144,512]{2,1,0:T(8,128)S(1)}, u32[]{:S(2)}, u32[]{:S(2)}) collective-permute-start(f32[2,144,512]{2,1,0:T(8,128)S(1)} %get-tuple-element.49.part_1.b_1), channel_id=1, source_target_pairs={{0,1},{1,2},{2,3},{3,4},{4,5},{5,6},{6,7},{7,8},{8,9},{9,10},{10,1... | collective-permute-start | bytes 1769480 | tf_op jit(solution)/shard_map/ppermute | solution.py:305
  225.3 4.3 %copy-start.32 = (f32[2,144,512]{2,1,0:T(8,128)}, f32[2,144,512]{2,1,0:T(8,128)S(1)}, u32[]{:S(2)}) copy-start(f32[2,144,512]{2,1,0:T(8,128)S(1)} %collective-permute-done.10.part_2.b_2) | copy-start | bytes 1769476
  227.4 9.8 %copy-start.44 = (f32[4,144,512]{2,1,0:T(8,128)}, f32[4,144,512]{2,1,0:T(8,128)S(1)}, u32[]{:S(2)}) copy-start(f32[4,144,512]{2,1,0:T(8,128)S(1)} %get-tuple-element.63.image_ref) | copy-start | bytes 3538948
  231.4 7.4 %copy-start.48 = (f32[8,128]{1,0:T(8,128)}, f32[8,128]{1,0:T(8,128)S(1)}, u32[]{:S(2)}) copy-start(f32[8,128]{1,0:T(8,128)S(1)} %get-tuple-element.74) | copy-start | bytes 12292
  231.4 48.0 %copy-start.6 = (f32[4,144,512]{2,1,0:T(8,128)S(1)}, f32[4,144,512]{2,1,0:T(8,128)}, u32[]{:S(2)}) copy-start(f32[4,144,512]{2,1,0:T(8,128)} %copy-done.5) | copy-start | bytes 3538948
  285.0 3.1 copy-start.19
  285.0 3.1 copy-start.21
  285.0 3.1 copy-start.43
  285.0 3.1 copy-start.53
  288.1 51.9 %collective-permute-start.11 = (f32[2,4,128,256]{3,2,1,0:T(8,128)}, f32[2,4,128,256]{3,2,1,0:T(8,128)}, u32[]{:S(2)}, u32[]{:S(2)}) collective-permute-start(f32[2,4,128,256]{3,2,1,0:T(8,128)} %get-tuple-element.65), channel_id=1, source_target_pairs={{0,16},{16,0},{1,17},{17,1},{2,18},{18,2},{3,19},{19,3},{4,20},{20... | collective-permute-start | bytes 3145736 | tf_op jit(solution)/shard_map/ppermute | solution.py:316
  288.2 3.6 %copy-start.9 = (f32[2,144,512]{2,1,0:T(8,128)S(1)}, f32[2,144,512]{2,1,0:T(8,128)}, u32[]{:S(2)}) copy-start(f32[2,144,512]{2,1,0:T(8,128)} %copy-done.7) | copy-start | bytes 1769476
  288.2 3.6 %copy-start.23 = (f32[2,144,512]{2,1,0:T(8,128)S(1)}, f32[2,144,512]{2,1,0:T(8,128)}, u32[]{:S(2)}) copy-start(f32[2,144,512]{2,1,0:T(8,128)} %copy-done.22) | copy-start | bytes 1769476
  288.2 3.6 %copy-start.25 = (f32[2,144,512]{2,1,0:T(8,128)S(1)}, f32[2,144,512]{2,1,0:T(8,128)}, u32[]{:S(2)}) copy-start(f32[2,144,512]{2,1,0:T(8,128)} %copy-done.24) | copy-start | bytes 1769476
  288.2 3.6 %copy-start.27 = (f32[2,144,512]{2,1,0:T(8,128)S(1)}, f32[2,144,512]{2,1,0:T(8,128)}, u32[]{:S(2)}) copy-start(f32[2,144,512]{2,1,0:T(8,128)} %copy-done.26) | copy-start | bytes 1769476
  288.2 3.6 %copy-start.41 = (f32[4,144,512]{2,1,0:T(8,128)S(1)}, f32[4,144,512]{2,1,0:T(8,128)}, u32[]{:S(2)}) copy-start(f32[4,144,512]{2,1,0:T(8,128)} %copy-done.40) | copy-start | bytes 3538948
  288.2 3.6 %copy-start.52 = (f32[8,128]{1,0:T(8,128)S(1)}, f32[8,128]{1,0:T(8,128)}, u32[]{:S(2)}) copy-start(f32[8,128]{1,0:T(8,128)} %get-tuple-element.83.dots_1) | copy-start | bytes 12292
  291.3 50.2 %collective-permute-start.16 = (f32[2,4,128,256]{3,2,1,0:T(8,128)}, f32[2,4,128,256]{3,2,1,0:T(8,128)}, u32[]{:S(2)}, u32[]{:S(2)}) collective-permute-start(f32[2,4,128,256]{3,2,1,0:T(8,128)} %get-tuple-element.77), channel_id=1, source_target_pairs={{0,16},{16,0},{1,17},{17,1},{2,18},{18,2},{3,19},{19,3},{4,20},{20... | collective-permute-start | bytes 3145736 | tf_op jit(solution)/shard_map/ppermute | solution.py:316
  297.2 45.9 %collective-permute-start.6 = (f32[2,4,128,256]{3,2,1,0:T(8,128)}, f32[2,4,128,256]{3,2,1,0:T(8,128)S(1)}, u32[]{:S(2)}, u32[]{:S(2)}) collective-permute-start(f32[2,4,128,256]{3,2,1,0:T(8,128)} %get-tuple-element.53), channel_id=1, source_target_pairs={{0,16},{16,0},{1,17},{17,1},{2,18},{18,2},{3,19},{19,3},{4,20},{20... | collective-permute-start | bytes 3145736 | tf_op jit(solution)/shard_map/ppermute | solution.py:316
  (25 other events, 33.9 us)
